TPU v7x, 256 devices: a whole 4x4x8 slice. The times are simulated.
256 devices in a mesh: grp: 16 (over y, x), ep: 16 (over z, core).
Axes of the slice: x: 4, y: 4, z: 8, core: 2. Of those that a mesh axis runs over, the one named last changes fastest.
Arguments:
- tokens: bfloat16 [24576, 4096], P(('grp', 'ep')), may hold values from -6 to 6
- hash_expert: int32 [24576, 1], P(('grp', 'ep')), may hold values from 0 to 15, as said below
- gate_weight: bfloat16 [16, 4096, 4096], P('ep', None, 'grp'), may hold values from -0.09375 to 0.09375
- up_weight: bfloat16 [16, 4096, 4096], P('ep', None, 'grp'), may hold values from -0.09375 to 0.09375
- down_weight: bfloat16 [16, 4096, 4096], P('ep', 'grp'), may hold values from -0.09375 to 0.09375
Outputs:
- combined: bfloat16 [24576, 4096], P(('grp', 'ep'))
- expert_load: float32 [16], replicated
- balance: float32 [], replicated
Inputs may be any that keep to these rules, and one draw needn't show every extreme that they name: `hash_expert`: among the 96 rows of one device no expert is named more than 9 times; on every device some expert is named exactly 9 times; every expert is named by some row.
All inputs are finite; a program needn't handle non-finite values.
Results may differ from a plain program's by a relative error of at most 0.014.
Values may be sent and summed in bfloat16 or wider, within the bound.
A program may use at most 128 MiB of HBM per device.

v0:
```python
import jax
import jax.numpy as jnp
from jax import lax
from jax.sharding import Mesh
from jax.sharding import PartitionSpec as P

EP = ("ep_0", "ep_1")
GRP = ("grp_0", "grp_1")
GRP_EP = ("grp_0", "grp_1", "ep_0", "ep_1")
eps = 1e-06


def one_axis_at_a_time(array, axes):
    for axis in axes:
        array = lax.psum(array, axis)
    return array


def body(tokens, hash_expert, gate_weight, up_weight, down_weight):
    tok_dev, model_width = tokens.shape
    local_experts = gate_weight.shape[0]
    ep_size = lax.axis_size(EP)
    grp_size = lax.axis_size(GRP)
    experts = local_experts * ep_size
    capacity = max(2, 3 * tok_dev // (2 * experts))
    raw_values = tokens.astype(jnp.float32)
    normed = (
        raw_values * lax.rsqrt(jnp.mean(raw_values * raw_values, axis=-1, keepdims=True) + eps)
    ).astype(jnp.bfloat16)
    expert = hash_expert[:, 0]
    onehot = expert[:, None] == jnp.arange(experts, dtype=jnp.int32)[None, :]
    onehot_int = onehot.astype(jnp.int32)
    slot_index = jnp.sum((jnp.cumsum(onehot_int, axis=0) - 1) * onehot_int, axis=1)
    target = expert * capacity + slot_index
    placing = (jnp.arange(experts * capacity, dtype=jnp.int32)[:, None] == target[None, :]).astype(
        jnp.bfloat16
    )
    packed = jnp.dot(placing, normed, preferred_element_type=jnp.float32).astype(jnp.bfloat16)
    packed = packed.reshape(ep_size, local_experts, capacity, model_width)
    received = lax.all_to_all(packed, EP, split_axis=0, concat_axis=0, tiled=True)
    block_rows = lax.all_gather(received, GRP, axis=0, tiled=True)
    gate_out = jnp.einsum(
        "secd,edf->secf", block_rows, gate_weight, preferred_element_type=jnp.float32
    )
    up_out = jnp.einsum("secd,edf->secf", block_rows, up_weight, preferred_element_type=jnp.float32)
    hidden = (jax.nn.silu(gate_out) * up_out).astype(jnp.bfloat16)
    summed = lax.psum_scatter(
        jnp.einsum(
            "secf,efd->secd", hidden, down_weight, preferred_element_type=jnp.float32
        ).astype(jnp.bfloat16),
        GRP,
        scatter_dimension=0,
        tiled=True,
    )
    returned_rows = lax.all_to_all(summed, EP, split_axis=0, concat_axis=1, tiled=True)
    returned = returned_rows.reshape(experts * capacity, model_width)
    combined = jnp.dot(placing.T, returned, preferred_element_type=jnp.float32).astype(jnp.bfloat16)
    counts = one_axis_at_a_time(jnp.sum(onehot.astype(jnp.float32), axis=0), GRP_EP)
    expert_load = counts * experts / (tok_dev * grp_size * ep_size)
    balance = jnp.sum(expert_load * expert_load) / experts
    return (combined, expert_load, balance)


def solution(mesh):
    split = Mesh(mesh.devices.reshape(4, 4, 8, 2), ("grp_0", "grp_1", "ep_0", "ep_1"))
    placed = (
        P(GRP_EP, None),
        P(GRP_EP, None),
        P(EP, None, GRP),
        P(EP, None, GRP),
        P(EP, GRP, None),
    )
    return jax.shard_map(
        body, mesh=split, in_specs=placed, out_specs=(P(GRP_EP, None), P(), P()), check_vma=False
    )
```

profile of v0, /device:TPU:1, one launch (start us, length us, event | category | flops | bytes accessed | tf_op | source)
XLA Modules:
  0.0 449.0 jit_solution(12240543204433801340)
XLA Ops:
  7.2 0.0 copy-start
  7.2 0.0 all-gather.2.cloned.1.call-start
  7.2 0.9 fusion.25
  8.1 0.1 reduce_window_sum.11
  8.2 0.8 select_reduce_fusion
  9.1 0.7 multiply_add_fusion
  9.7 1.4 fusion.11
  11.2 1.7 convolution_convert_fusion
  12.8 1.6 reshape.52
  14.5 60.9 %all_to_all.14 = bf16[16,1,9,4096]{3,2,1,0:T(8,128)(2,1)S(1)} all-to-all(bf16[16,1,9,4096]{3,2,1,0:T(8,128)(2,1)} %bitcast.69), channel_id=1, replica_groups=mesh['grp_0'=4,'grp_1'=4,'ep_0'=8,'ep_1'=2] {'ep_0','ep_1'}, dimensions={0} | all-to-all | bytes 2359296 | tf_op jit(solution)/shard_map/all_to_all | solution.py:40
  75.3 1.8 copy.12
  77.1 0.0 all-gather.2.cloned.1.call-update
  77.1 0.0 reduce-scatter.2.cloned.1.call-start
  77.2 123.7 %all-gather.2.cloned.1.call-done = bf16[256,1,9,4096]{3,0,2,1:T(8,128)(2,1)} async-done(((bf16[16,1,9,4096]{3,0,2,1:T(8,128)(2,1)}), bf16[256,1,9,4096]{3,0,2,1:T(8,128)(2,1)}) %all-gather.2.cloned.1.call-update) | async-done | bytes 18874384 | tf_op jit(solution)/shard_map/all_gather | solution.py:41
  200.8 10.6 %fusion = f32[256,9,256]{2,0,1:T(8,128)} fusion(bf16[256,1,9,4096]{3,0,2,1:T(8,128)(2,1)} %all-gather.2.cloned.1.call-done, bf16[1,4096,256]{2,1,0:T(8,128)(2,1)} %param.8), kind=kOutput, calls=%fused_computation | convolution fusion | flops 4831838208 | bytes 23330816 | tf_op jit(solution)/shard_map/secd,edf->secf/dot_general | solution.py:45
  211.4 0.0 copy-done
  211.4 26.2 %convert_bitcast_fusion = bf16[256,1,9,4096]{3,0,2,1:T(8,128)(2,1)} fusion(bf16[1,256,4096]{2,1,0:T(8,128)(2,1)S(1)} %copy-done, f32[256,9,256]{2,0,1:T(8,128)} %fusion, bf16[256,1,9,4096]{3,0,2,1:T(8,128)(2,1)} %all-gather.2.cloned.1.call-done, bf16[1,4096,256]{2,1,0:T(8,128)(2,1)} %param.7), kind=kOutput, calls=%fused_computation.4 | convolution fusion | flops 9676652544 | bytes 44302336 | tf_op jit(solution)/shard_map/secf,efd->secd/dot_general | solution.py:48
  237.6 0.0 reduce-scatter.2.cloned.1.call-update
  237.6 125.7 %reduce-scatter.2.cloned.1.call-done = bf16[16,1,9,4096]{3,0,2,1:T(8,128)(2,1)} async-done(((bf16[256,1,9,4096]{3,0,2,1:T(8,128)(2,1)}), bf16[16,1,9,4096]{3,0,2,1:T(8,128)(2,1)}) %reduce-scatter.2.cloned.1.call-update) | async-done | bytes 1179664 | tf_op jit(solution)/shard_map/reduce_scatter | solution.py:47
  363.3 3.4 copy.13
  366.7 0.0 copy-start.1
  366.7 8.3 %all-to-all-start.1 = ((bf16[16,1,9,4096]{3,2,1,0:T(8,128)(2,1)}), bf16[16,1,9,4096]{3,2,1,0:T(8,128)(2,1)}, u32[]{:S(2)}, u32[]{:S(2)}) async-start(bf16[16,1,9,4096]{3,2,1,0:T(8,128)(2,1)} %copy.13), calls=%async_computation.2 | async-start | bytes 4194304 | tf_op jit(solution)/shard_map/all_to_all | solution.py:55
  375.0 0.0 copy-done.1
  375.0 0.1 convert_reduce_fusion
  375.1 8.8 %psum.28 = f32[16]{0:T(128)S(1)} all-reduce(f32[16]{0:T(128)S(1)} %convert_reduce_fusion), channel_id=1, replica_groups=mesh['grp_0'=4,'grp_1'=4,'ep_0'=8,'ep_1'=2] {'grp_0'}, use_global_device_ids=true, to_apply=%region_5.6 | all-reduce | flops 16 | bytes 128 | tf_op jit(solution)/shard_map/psum | solution.py:15
  383.9 7.4 %psum.29 = f32[16]{0:T(128)S(1)} all-reduce(f32[16]{0:T(128)S(1)} %psum.28), channel_id=1, replica_groups=mesh['grp_0'=4,'grp_1'=4,'ep_0'=8,'ep_1'=2] {'grp_1'}, use_global_device_ids=true, to_apply=%region_6.7 | all-reduce | flops 16 | bytes 128 | tf_op jit(solution)/shard_map/psum | solution.py:15
  391.3 39.3 %psum.30 = f32[16]{0:T(128)S(1)} all-reduce(f32[16]{0:T(128)S(1)} %psum.29), channel_id=1, replica_groups=mesh['grp_0'=4,'grp_1'=4,'ep_0'=8,'ep_1'=2] {'ep_0'}, use_global_device_ids=true, to_apply=%region_7.8 | all-reduce | flops 16 | bytes 128 | tf_op jit(solution)/shard_map/psum | solution.py:15
  430.6 5.5 %psum.31 = f32[16]{0:T(128)S(1)} all-reduce(f32[16]{0:T(128)S(1)} %psum.30), channel_id=1, replica_groups=mesh['grp_0'=4,'grp_1'=4,'ep_0'=8,'ep_1'=2] {'ep_1'}, use_global_device_ids=true, to_apply=%region_8.9 | all-reduce | flops 16 | bytes 128 | tf_op jit(solution)/shard_map/psum | solution.py:15
  436.1 1.1 multiply_reduce_fusion
  437.9 0.0 all-to-all-done.1
  437.9 1.8 reshape.58
  439.7 1.3 convolution_convert_fusion.1
  (1 shorter events, 0.0 us)
Async XLA Ops:
  7.2 204.3 %copy-start = (bf16[1,256,4096]{2,1,0:T(8,128)(2,1)S(1)}, bf16[1,256,4096]{2,1,0:T(8,128)(2,1)}, u32[]{:S(2)}) copy-start(bf16[1,256,4096]{2,1,0:T(8,128)(2,1)} %param.9) | copy-start | bytes 6291460
  7.2 193.7 %all-gather.2.cloned.1.call-start = ((), (), s32[]{:S(2)}) async-start(), calls=%async_computation.3 | async-start | bytes 20054016 | tf_op jit(solution)/shard_map/all_gather | solution.py:41
  77.1 286.2 %reduce-scatter.2.cloned.1.call-start = ((), (), s32[]{:S(2)}) async-start(), calls=%async_computation.4 | async-start | bytes 20054016 | tf_op jit(solution)/shard_map/reduce_scatter | solution.py:47
  366.7 8.3 %copy-start.1 = (s32[96,1]{0,1:T(1,128)S(1)}, s32[96,1]{0,1:T(1,128)}, u32[]{:S(2)}) copy-start(s32[96,1]{0,1:T(1,128)} %param.6) | copy-start | bytes 1156
  366.7 71.2 %all-to-all-start.1 = ((bf16[16,1,9,4096]{3,2,1,0:T(8,128)(2,1)}), bf16[16,1,9,4096]{3,2,1,0:T(8,128)(2,1)}, u32[]{:S(2)}, u32[]{:S(2)}) async-start(bf16[16,1,9,4096]{3,2,1,0:T(8,128)(2,1)} %copy.13), calls=%async_computation.2 | async-start | bytes 4194304 | tf_op jit(solution)/shard_map/all_to_all | solution.py:55
Sparse Core Ops, SparseCore 0:
  77.2 123.5 all-gather.1
  237.8 125.5 reduce-scatter.1
where the time goes:
time: 449 us
  waiting for transfers between devices  249 us (55%)
  blocking collectives  122 us (27%)
  matrix products  39.8 us (9%)
  between operations  15.9 us (4%)
  local copies, waits for them, and re-layouts  8.61 us (2%)
  starting transfers between devices  8.38 us (2%)
  other arithmetic  5.11 us (1%)
    reduce_scatter x1, waiting for transfers between devices, body(): lax.psum_scatter(jnp.einsum('secf,efd->secd', hidden, down_weight, prefer...  126 us
    all_gather x1, waiting for transfers between devices, body(): block_rows = lax.all_gather(received, GRP, axis=0, tiled=True)  124 us
    psum x4, blocking collectives, one_axis_at_a_time(): array = lax.psum(array, axis)  61 us
    all_to_all x1, blocking collectives, body(): lax.all_to_all(packed, EP, split_axis=0, concat_axis=0, tiled=True)  60.9 us
    dot_general x1, matrix products, body(): jnp.einsum('secf,efd->secd', hidden, down_weight, preferred_element_type=...  26.2 us
    dot_general x1, matrix products, body(): jnp.einsum('secd,edf->secf', block_rows, up_weight, preferred_element_typ...  10.6 us
  transfers between devices with their start and end apart: 3, of which 2 were waited for; matrix products, arithmetic and copies ran while one was open for 0% of the time, Pallas kernels for 0%

commit v1 on v0

--- a/solution.py
+++ b/solution.py
@@ -38,7 +38,9 @@
     packed = jnp.dot(placing, normed, preferred_element_type=jnp.float32).astype(jnp.bfloat16)
     packed = packed.reshape(ep_size, local_experts, capacity, model_width)
     received = lax.all_to_all(packed, EP, split_axis=0, concat_axis=0, tiled=True)
-    block_rows = lax.all_gather(received, GRP, axis=0, tiled=True)
+    block_rows = jnp.concatenate(
+        lax.all_to_all(jnp.stack([received] * lax.axis_size(GRP)), GRP, 0, 0), axis=0
+    )
     gate_out = jnp.einsum(
         "secd,edf->secf", block_rows, gate_weight, preferred_element_type=jnp.float32
     )

time: 449 us -> 542 us (1.21)
  blocking collectives: 122 us -> 338 us
  waiting for transfers between devices: 249 us -> 119 us
  local copies, waits for them, and re-layouts: 8.61 us -> 16.4 us
    all_to_all x0 -> x1, blocking collectives: none -> 216 us  [body(): lax.all_to_all(jnp.stack([received] * lax.axis_size(GRP)), GRP, 0, 0)]
    all_gather x1 -> x0, waiting for transfers between devices: 124 us -> none  [body(): block_rows = lax.all_gather(received, GRP, axis=0, tiled=True)]
    reduce_scatter x1, waiting for transfers between devices: 126 us -> 119 us  [body(): lax.psum_scatter(jnp.einsum('secf,efd->secd', hidden, down_weight, prefer...]
    all_to_all x0 -> x1, local copies, waits for them, and re-layouts: none -> 6.6 us  [body(): lax.all_to_all(jnp.stack([received] * lax.axis_size(GRP)), GRP, 0, 0)]
  transfers between devices with their start and end apart: 3 -> 2, of which waited for: 2 -> 1; matrix products, arithmetic and copies ran while one was open for 0% -> 0% of each run, Pallas kernels for 0% -> 0%
where the time goes in v1:
time: 542 us
  blocking collectives  338 us (62%)
  waiting for transfers between devices  119 us (22%)
  matrix products  39.5 us (7%)
  local copies, waits for them, and re-layouts  16.4 us (3%)
  between operations  15.9 us (3%)
  starting transfers between devices  8.31 us (2%)
    all_to_all x1, blocking collectives, body(): lax.all_to_all(jnp.stack([received] * lax.axis_size(GRP)), GRP, 0, 0)  216 us
    reduce_scatter x1, waiting for transfers between devices, body(): lax.psum_scatter(jnp.einsum('secf,efd->secd', hidden, down_weight, prefer...  119 us
    psum x4, blocking collectives, one_axis_at_a_time(): array = lax.psum(array, axis)  61 us
    all_to_all x1, blocking collectives, body(): lax.all_to_all(packed, EP, split_axis=0, concat_axis=0, tiled=True)  60.9 us
    dot_general x1, matrix products, body(): jnp.einsum('secf,efd->secd', hidden, down_weight, preferred_element_type=...  26.1 us
  transfers between devices with their start and end apart: 2, of which 1 were waited for; matrix products, arithmetic and copies ran while one was open for 0% of the time, Pallas kernels for 0%

profile of v1, /device:TPU:1, one launch (start us, length us, event | category | flops | bytes accessed | tf_op | source)
XLA Modules:
  0.0 541.6 jit_solution(9462351243214822090)
XLA Ops:
  7.2 0.0 copy-start
  7.2 0.0 reduce-scatter.2.cloned.1.call-start
  7.2 0.9 fusion.21
  8.1 0.1 reduce_window_sum.11
  8.2 0.8 select_reduce_fusion
  9.1 0.7 multiply_add_fusion
  9.7 1.4 fusion.9
  11.2 1.7 convolution_convert_fusion
  12.8 1.6 reshape.58
  14.5 60.9 %all_to_all.22 = bf16[16,1,9,4096]{3,2,1,0:T(8,128)(2,1)S(1)} all-to-all(bf16[16,1,9,4096]{3,2,1,0:T(8,128)(2,1)} %bitcast.71), channel_id=1, replica_groups=mesh['grp_0'=4,'grp_1'=4,'ep_0'=8,'ep_1'=2] {'ep_0','ep_1'}, dimensions={0} | all-to-all | bytes 2359296 | tf_op jit(solution)/shard_map/all_to_all | solution.py:40
  75.3 0.7 copy.12
  76.1 2.2 stack.2
  78.3 216.1 %all_to_all.23 = bf16[16,16,1,9,4096]{4,1,3,2,0:T(8,128)(2,1)S(1)} all-to-all(bf16[16,16,1,9,4096]{4,1,3,2,0:T(8,128)(2,1)S(1)} %stack.2), channel_id=1, replica_groups=mesh['grp_0'=4,'grp_1'=4,'ep_0'=8,'ep_1'=2] {'grp_0','grp_1'}, dimensions={0} | all-to-all | bytes 37748736 | tf_op jit(solution)/shard_map/all_to_all | solution.py:42
  294.4 0.0 copy-start.2
  294.4 6.6 %copy.13 = bf16[16,16,1,9,4096]{4,1,0,3,2:T(8,128)(2,1)} copy(bf16[16,16,1,9,4096]{4,1,3,2,0:T(8,128)(2,1)S(1)} %all_to_all.23) | data formatting | bytes 37748736 | tf_op jit(solution)/shard_map/all_to_all | solution.py:42
  301.0 0.0 copy-done.2
  301.0 10.4 %fusion.5 = f32[256,9,256]{2,0,1:T(8,128)} fusion(bf16[256,9,4096]{2,0,1:T(8,128)(2,1)} %bitcast.69, bf16[1,4096,256]{2,1,0:T(8,128)(2,1)S(1)} %copy-done.2), kind=kOutput, calls=%fused_computation.11 | convolution fusion | flops 4831838208 | bytes 23330816 | tf_op jit(solution)/shard_map/secd,edf->secf/dot_general | solution.py:47
  311.3 0.0 copy-done
  311.3 26.1 %convert_bitcast_fusion = bf16[256,1,9,4096]{3,0,2,1:T(8,128)(2,1)} fusion(bf16[1,256,4096]{2,1,0:T(8,128)(2,1)S(1)} %copy-done, f32[256,9,256]{2,0,1:T(8,128)} %fusion.5, bf16[256,9,4096]{2,0,1:T(8,128)(2,1)} %bitcast.70, bf16[1,4096,256]{2,1,0:T(8,128)(2,1)} %param.7), kind=kOutput, calls=%fused_computation | convolution fusion | flops 9676652544 | bytes 44302336 | tf_op jit(solution)/shard_map/secf,efd->secd/dot_general | solution.py:50
  337.4 0.0 reduce-scatter.2.cloned.1.call-update
  337.5 118.5 %reduce-scatter.2.cloned.1.call-done = bf16[16,1,9,4096]{3,0,2,1:T(8,128)(2,1)} async-done(((bf16[256,1,9,4096]{3,0,2,1:T(8,128)(2,1)}), bf16[16,1,9,4096]{3,0,2,1:T(8,128)(2,1)}) %reduce-scatter.2.cloned.1.call-update) | async-done | bytes 1179664 | tf_op jit(solution)/shard_map/reduce_scatter | solution.py:49
  456.0 3.4 copy.14
  459.4 0.0 copy-start.1
  459.4 8.3 %all-to-all-start.2 = ((bf16[16,1,9,4096]{3,2,1,0:T(8,128)(2,1)}), bf16[16,1,9,4096]{3,2,1,0:T(8,128)(2,1)}, u32[]{:S(2)}, u32[]{:S(2)}) async-start(bf16[16,1,9,4096]{3,2,1,0:T(8,128)(2,1)} %copy.14), calls=%async_computation.3 | async-start | bytes 4194304 | tf_op jit(solution)/shard_map/all_to_all | solution.py:57
  467.7 0.0 copy-done.1
  467.7 0.1 convert_reduce_fusion
  467.8 8.8 %psum.28 = f32[16]{0:T(128)S(1)} all-reduce(f32[16]{0:T(128)S(1)} %convert_reduce_fusion), channel_id=1, replica_groups=mesh['grp_0'=4,'grp_1'=4,'ep_0'=8,'ep_1'=2] {'grp_0'}, use_global_device_ids=true, to_apply=%region_5.6 | all-reduce | flops 16 | bytes 128 | tf_op jit(solution)/shard_map/psum | solution.py:15
  476.5 7.4 %psum.29 = f32[16]{0:T(128)S(1)} all-reduce(f32[16]{0:T(128)S(1)} %psum.28), channel_id=1, replica_groups=mesh['grp_0'=4,'grp_1'=4,'ep_0'=8,'ep_1'=2] {'grp_1'}, use_global_device_ids=true, to_apply=%region_6.7 | all-reduce | flops 16 | bytes 128 | tf_op jit(solution)/shard_map/psum | solution.py:15
  483.9 39.3 %psum.30 = f32[16]{0:T(128)S(1)} all-reduce(f32[16]{0:T(128)S(1)} %psum.29), channel_id=1, replica_groups=mesh['grp_0'=4,'grp_1'=4,'ep_0'=8,'ep_1'=2] {'ep_0'}, use_global_device_ids=true, to_apply=%region_7.8 | all-reduce | flops 16 | bytes 128 | tf_op jit(solution)/shard_map/psum | solution.py:15
  523.2 5.5 %psum.31 = f32[16]{0:T(128)S(1)} all-reduce(f32[16]{0:T(128)S(1)} %psum.30), channel_id=1, replica_groups=mesh['grp_0'=4,'grp_1'=4,'ep_0'=8,'ep_1'=2] {'ep_1'}, use_global_device_ids=true, to_apply=%region_8.9 | all-reduce | flops 16 | bytes 128 | tf_op jit(solution)/shard_map/psum | solution.py:15
  528.8 1.1 multiply_reduce_fusion
  530.5 0.0 all-to-all-done.2
  530.5 1.8 reshape.64
  532.4 1.3 convolution_convert_fusion.1
  (1 shorter events, 0.0 us)
Async XLA Ops:
  7.2 304.2 %copy-start = (bf16[1,256,4096]{2,1,0:T(8,128)(2,1)S(1)}, bf16[1,256,4096]{2,1,0:T(8,128)(2,1)}, u32[]{:S(2)}) copy-start(bf16[1,256,4096]{2,1,0:T(8,128)(2,1)} %param.9) | copy-start | bytes 6291460
  7.2 448.8 %reduce-scatter.2.cloned.1.call-start = ((), (), s32[]{:S(2)}) async-start(), calls=%async_computation.4 | async-start | bytes 20054016 | tf_op jit(solution)/shard_map/reduce_scatter | solution.py:49
  294.4 6.6 %copy-start.2 = (bf16[1,4096,256]{2,1,0:T(8,128)(2,1)S(1)}, bf16[1,4096,256]{2,1,0:T(8,128)(2,1)}, u32[]{:S(2)}) copy-start(bf16[1,4096,256]{2,1,0:T(8,128)(2,1)} %param.8) | copy-start | bytes 6291460
  459.4 8.3 %copy-start.1 = (s32[96,1]{0,1:T(1,128)S(1)}, s32[96,1]{0,1:T(1,128)}, u32[]{:S(2)}) copy-start(s32[96,1]{0,1:T(1,128)} %param.6) | copy-start | bytes 1156
  459.4 71.1 %all-to-all-start.2 = ((bf16[16,1,9,4096]{3,2,1,0:T(8,128)(2,1)}), bf16[16,1,9,4096]{3,2,1,0:T(8,128)(2,1)}, u32[]{:S(2)}, u32[]{:S(2)}) async-start(bf16[16,1,9,4096]{3,2,1,0:T(8,128)(2,1)} %copy.14), calls=%async_computation.3 | async-start | bytes 4194304 | tf_op jit(solution)/shard_map/all_to_all | solution.py:57
Sparse Core Ops, SparseCore 0:
  337.6 118.3 reduce-scatter.1
